TPU v7x, 32 devices: a whole 2x2x4 slice. The times are simulated.
32 devices in a mesh: grp: 2 (over x), seq: 4 (over y, core), tp: 4 (over z).
Axes of the slice: x: 2, y: 2, z: 4, core: 2. Of those that a mesh axis runs over, the one named last changes fastest.
Arguments:
- hidden: bfloat16 [2, 1024, 4096], P('grp', 'seq'), may hold values from -72 to 72
- w_query: bfloat16 [4096, 2048], P('seq', 'tp'), may hold values from -0.09375 to 0.09375
- w_key: bfloat16 [4096, 2048], P('seq', 'tp'), may hold values from -0.09375 to 0.09375
- w_value: bfloat16 [4096, 2048], P('seq', 'tp'), may hold values from -0.09375 to 0.09375
- prompt_len: int32 [256], replicated, may hold values from 1 to 1024
- page_table: int32 [256, 32], replicated, may hold values from 0 to 63, all different within a row
Outputs:
- attended: bfloat16 [2, 1024, 2048], P('grp', 'seq', 'tp')
Inputs may be any that keep to these rules, and one draw needn't show every extreme that they name: `page_table`: every row lists 32 different pages; every page is listed by some row.
All inputs are finite; a program needn't handle non-finite values.
Results may differ from a plain program's by a relative error of at most 0.006.
The roundings to bfloat16 on the way count: a program that leaves them out, or rounds other values in their place, can miss the bound.
Values may be sent and summed in bfloat16 or wider, within the bound.
A program may use at most 128 MiB of HBM per device.

v0:
```python
import math

import jax
import jax.numpy as jnp
from jax import lax
from jax.experimental import pallas as pl
from jax.experimental.pallas import tpu as pltpu
from jax.sharding import PartitionSpec as P

HD = 128
PAGE = 16
STEPS = 4


NEG = -1e30


def from_behind(value, axis, steps):
    count = lax.axis_size(axis)
    first, last = (max(0, -steps), min(count, count - steps))
    return lax.ppermute(value, axis, [(source, source + steps) for source in range(first, last)])


def partial_attention(query, keys, values, allowed):
    rows = query.shape[0]
    heads = query.shape[1] // HD
    query_heads = query.reshape(rows, heads, HD)
    key_heads = keys.reshape(keys.shape[0], heads, HD)
    value_heads = values.reshape(values.shape[0], heads, HD)
    scores = jnp.einsum(
        "rhd,shd->hrs", query_heads, key_heads, preferred_element_type=jnp.float32
    ) * HD ** (-0.5)
    scores = jnp.where(allowed[None], scores, NEG)
    top = jnp.max(scores, axis=2)
    weights = jnp.where(allowed[None], jnp.exp(scores - top[:, :, None]), 0.0)
    total = jnp.sum(weights, axis=2)
    summed = jnp.einsum(
        "hrs,shd->rhd",
        weights.astype(jnp.bfloat16),
        value_heads,
        preferred_element_type=jnp.float32,
    )
    return (top, total, summed.reshape(rows, heads * HD))


def rescale(summed, factor):
    rows = summed.shape[0]
    heads = factor.shape[0]
    return (summed.reshape(rows, heads, HD) * factor.T[:, :, None]).reshape(rows, heads * HD)


def combine(first, second):
    top = jnp.maximum(first[0], second[0])
    early = jnp.exp(first[0] - top)
    later = jnp.exp(second[0] - top)
    return (
        top,
        first[1] * early + second[1] * later,
        rescale(first[2], early) + rescale(second[2], later),
    )


def finish(state):
    return rescale(state[2], 1.0 / state[1]).astype(jnp.bfloat16)


def row_mask(tables, lengths, key_pos):
    pages = key_pos // PAGE
    member = jnp.any(tables[:, :, None] == pages[None, None, :], axis=1)
    allowed = member & (key_pos[None, :] < lengths[:, None])
    return jnp.repeat(allowed, STEPS, axis=0)


def blocked(carry, keys, values, query, mask_of):
    count = keys.shape[0]
    block = math.gcd(count, 512)

    def one_block(state, offset):
        piece_keys = lax.dynamic_slice_in_dim(keys, offset, block, 0)
        piece_values = lax.dynamic_slice_in_dim(values, offset, block, 0)
        key_pos = offset + jnp.arange(block)
        return (
            combine(state, partial_attention(query, piece_keys, piece_values, mask_of(key_pos))),
            None,
        )

    offsets = jnp.arange(count // block) * block
    state, unused = lax.scan(one_block, carry, offsets)
    return state


def on_device(hidden, w_query, w_key, w_value, prompt_len, page_table):
    local = hidden[0]
    rows = local.shape[0]
    width = w_query.shape[1]
    heads = width // HD
    seq_index = lax.axis_index("seq")
    is_prompt = lax.axis_index("grp") == 0
    empty = jnp.zeros((rows, width), jnp.float32)
    piece = (
        lax.all_gather(w_query, "seq", axis=0, tiled=True),
        lax.all_gather(w_key, "seq", axis=0, tiled=True),
        lax.all_gather(w_value, "seq", axis=0, tiled=True),
    )
    projected = tuple(
        (jnp.dot(local, weight, preferred_element_type=jnp.float32) for weight in piece)
    )
    query, keys, values = [item.astype(jnp.bfloat16) for item in projected]
    positions = seq_index * rows + jnp.arange(rows)
    start_state = (
        jnp.full((heads, rows), NEG, jnp.float32),
        jnp.zeros((heads, rows), jnp.float32),
        empty,
    )
    given_keys, given_values = from_behind((keys, values), "grp", 1)
    cache_keys = jnp.where(is_prompt, keys, given_keys)
    cache_values = jnp.where(is_prompt, values, given_values)
    row_count = rows // STEPS
    own_tables = lax.dynamic_slice_in_dim(page_table, seq_index * row_count, row_count, 0)
    own_lengths = lax.dynamic_slice_in_dim(prompt_len, seq_index * row_count, row_count, 0)

    def mask_of(key_pos):
        causal = key_pos[None, :] <= positions[:, None]
        listed = row_mask(own_tables, own_lengths, key_pos)
        return jnp.where(is_prompt, causal, listed)

    piece = (
        lax.all_gather(cache_keys, "seq", axis=0, tiled=True),
        lax.all_gather(cache_values, "seq", axis=0, tiled=True),
    )
    state = blocked(start_state, piece[0], piece[1], query, mask_of)
    frame_row = positions // STEPS
    own_rows = (frame_row[:, None] == frame_row[None, :]) & (
        positions[None, :] <= positions[:, None]
    )
    fresh = partial_attention(query, keys, values, own_rows)
    prefill_out = finish(state)
    decode_out = finish(combine(state, fresh))
    return jnp.where(is_prompt, prefill_out, decode_out)[None]


QUERY, KEY, VALUE = 0, 1, 2
ORDER = (KEY, VALUE, QUERY)
SUBS = 1
LAG = 1
PARTS = 2


def fused_kernel(
    hidden, w_query, w_key, w_value, lengths_in, tables_in, out,
    lengths, tables, hbuf, near, far, far_q, acc, qbuf, fresh, cache, bias, osend, orecv,
    y_send, y_recv, x_send, x_recv, d_send, d_recv, local_sem,
    kx_send, kx_recv, ky_send, ky_recv, o_send, o_recv,
):
    weights = {QUERY: w_query, KEY: w_key, VALUE: w_value}
    rows = hidden.shape[1]
    depth = w_query.shape[0]
    half = w_query.shape[1] // 2
    heads = half // HD
    chip_rows = 2 * rows
    grp = lax.axis_index("grp")
    seq = lax.axis_index("seq")
    y = seq // 2
    core = seq % 2
    partner = {"seq": 2 * y + 1 - core}
    across = [{"seq": 2 * (1 - y) + core}, {"seq": 2 * (1 - y) + 1 - core}]
    beside = {"grp": 1 - grp}
    core_of = [core, 1 - core]
    piece = depth // 2 // SUBS

    barrier = pltpu.get_barrier_semaphore()
    for other in (partner, across[0], across[1], beside):
        pl.semaphore_signal(barrier, inc=1, device_id=other, device_id_type=pl.DeviceIdType.MESH)
    pl.semaphore_wait(barrier, 4)

    def remote(src, dst, send, recv, to):
        return pltpu.make_async_remote_copy(
            src_ref=src, dst_ref=dst, send_sem=send, recv_sem=recv,
            device_id=to, device_id_type=pl.DeviceIdType.MESH,
        )

    def columns(which):
        return pl.ds(pl.multiple_of(core_of[which] * half, half), half)

    kv_steps = [(m, sub, rel) for m in (KEY, VALUE) for sub in range(SUBS) for rel in range(2)]
    q_steps = [(QUERY, head, rel) for head in range(heads) for rel in range(2)]
    steps = kv_steps + q_steps

    def slot(m, rel, way, sub):
        if m == QUERY:
            return (sub * 2 + rel) * 2 + way
        return (((m - KEY) * SUBS + sub) * 2 + rel) * 2 + way

    def landing(m, rel, way, sub):
        return (far_q if m == QUERY else far).at[slot(m, rel, way, sub)]

    def number(m, rel, way, sub):
        return slot(m, rel, way, sub) + (8 * SUBS if m == QUERY else 0)

    def weight_copy(m, sub, rel):
        if m == QUERY:
            span = pl.ds(pl.multiple_of(grp * (depth // 2), depth // 2), depth // 2)
            across_lanes = pl.ds(pl.multiple_of(core_of[rel] * half + sub * HD, HD), HD)
        else:
            span = pl.ds(pl.multiple_of(grp * (depth // 2) + sub * piece, piece), piece)
            across_lanes = columns(rel)
        at = number(m, rel, 0, sub)
        return remote(
            weights[m].at[span, across_lanes], landing(m, rel, 0, sub),
            y_send.at[at], y_recv.at[at], across[rel],
        )

    def forward_copy(m, sub, rel):
        at = number(m, rel, 1, sub)
        return remote(
            landing(m, rel, 0, sub), landing(m, rel, 1, sub), x_send.at[at], x_recv.at[at], beside
        )

    sent = []
    for step in steps:
        copy = weight_copy(*step)
        copy.start()
        sent.append(copy)
    my_rows = pl.ds(pl.multiple_of(core * rows, rows), rows)
    hidden_swap = remote(hidden.at[0], hbuf.at[my_rows], d_send.at[3], d_recv.at[3], partner)
    hidden_swap.start()
    swaps = {
        m: remote(weights[m].at[:, columns(1)], near.at[2 * m + 1], d_send.at[m], d_recv.at[m], partner)
        for m in ORDER
    }
    keeps = {
        m: pltpu.make_async_copy(weights[m].at[:, columns(0)], near.at[2 * m], local_sem.at[m])
        for m in ORDER
    }
    hidden_keep = pltpu.make_async_copy(hidden.at[0], hbuf.at[my_rows], local_sem.at[3])
    hidden_keep.start()
    for m in ORDER:
        keeps[m].start()
        swaps[m].start()
    sent += [hidden_swap] + [swaps[m] for m in ORDER]

    table_keep = pltpu.make_async_copy(tables_in, tables, local_sem.at[4])
    length_keep = pltpu.make_async_copy(lengths_in, lengths, local_sem.at[5])
    table_keep.start()
    length_keep.start()
    table_keep.wait()
    length_keep.wait()

    decode_rows = chip_rows // STEPS
    pages = 2 * chip_rows // PAGE
    own_rows = pl.ds(pl.multiple_of(y * decode_rows, decode_rows), decode_rows)
    own_table = tables[:, own_rows]
    own_length = lengths[:, own_rows]
    page_row = lax.broadcasted_iota(jnp.int32, (pages, decode_rows), 0)
    member = own_table[0:1, :] == page_row
    for listed in range(1, own_table.shape[0]):
        member = member | (own_table[listed : listed + 1, :] == page_row)
    member = jnp.where(member, 1.0, 0.0).astype(jnp.bfloat16)
    step_bits = STEPS.bit_length() - 1
    page_bits = PAGE.bit_length() - 1
    spread = (
        lax.shift_right_logical(lax.broadcasted_iota(jnp.int32, (chip_rows, decode_rows), 0), step_bits)
        == lax.broadcasted_iota(jnp.int32, (chip_rows, decode_rows), 1)
    )
    spread = jnp.where(spread, 1.0, 0.0).astype(jnp.bfloat16)
    prompt_one = jnp.where(grp == 0, 1, 0)
    contract_last = (((1,), (1,)), ((), ()))
    for side in range(2):
        base = (y if side == 0 else 1 - y) * chip_rows
        key_page = lax.shift_right_logical(
            lax.broadcasted_iota(jnp.int32, (chip_rows, pages), 0) + base, page_bits
        )
        unfold = lax.broadcasted_iota(jnp.int32, (chip_rows, pages), 1) == key_page
        unfold = jnp.where(unfold, 1.0, 0.0).astype(jnp.bfloat16)
        seen = jnp.dot(unfold, member, preferred_element_type=jnp.float32)
        key_pos = lax.broadcasted_iota(jnp.int32, (chip_rows, decode_rows), 0) + base
        seen = jnp.where(key_pos < own_length, seen, 0.0).astype(jnp.bfloat16)
        listed = lax.dot_general(spread, seen, contract_last, preferred_element_type=jnp.float32)
        causal = (
            lax.broadcasted_iota(jnp.int32, (chip_rows, chip_rows), 1) + base
            <= lax.broadcasted_iota(jnp.int32, (chip_rows, chip_rows), 0) + y * chip_rows
        )
        causal = jnp.where(causal, 1.0, 0.0)
        allowed = jnp.where(prompt_one == 1, causal, listed)
        bias[:, side * chip_rows : (side + 1) * chip_rows] = jnp.where(allowed > 0.5, 0.0, NEG)

    def add(m, weight, first, count, fresh_start=False):
        left = hbuf[:, pl.ds(pl.multiple_of(first, count), count)]
        product = jnp.dot(left, weight, preferred_element_type=jnp.float32)
        if fresh_start:
            acc[m] = product
        else:
            acc[m] += product

    hidden_keep.wait()
    hidden_swap.wait_recv()
    for m in ORDER:
        keeps[m].wait()
        add(m, near[2 * m], (2 * y + core) * depth, depth, True)
        swaps[m].wait_recv()
        add(m, near[2 * m + 1], (2 * y + 1 - core) * depth, depth)

    def from_across(m, sub, rel, way):
        owner = grp if way == 0 else 1 - grp
        first = (2 * (1 - y) + core_of[rel]) * depth + owner * (depth // 2)
        weight = landing(m, rel, way, sub)[...]
        if m != QUERY:
            add(m, weight, first + sub * piece, piece)
            return
        left = hbuf[:, pl.ds(pl.multiple_of(first, depth // 2), depth // 2)]
        acc[m, :, sub * HD : (sub + 1) * HD] += jnp.dot(
            left, weight, preferred_element_type=jnp.float32
        )

    def take_y(step):
        weight_copy(*step).wait_recv()
        copy = forward_copy(*step)
        copy.start()
        sent.append(copy)
        from_across(*step, 0)

    def take_x(step):
        forward_copy(*step).wait_recv()
        from_across(*step, 1)

    kv_pieces = [(kind, part) for kind in range(2) for part in range(PARTS)]
    part_rows = chip_rows // PARTS

    def piece_of(ref, at, part):
        return ref.at[at, pl.ds(part * part_rows, part_rows)]

    def kx_copy(kind, part):
        at = kind * PARTS + part
        return remote(
            piece_of(fresh, kind, part), piece_of(cache, kind, part), kx_send.at[at], kx_recv.at[at], beside
        )

    def ky_copy(kind, part, source):
        at = kind * PARTS + part
        return remote(
            piece_of(source, kind, part), piece_of(cache, 2 + kind, part),
            ky_send.at[at], ky_recv.at[at], across[0],
        )

    def settle(kind, m):
        fresh[kind] = acc[m].astype(jnp.bfloat16)

        @pl.when(grp == 0)
        def _():
            for part in range(PARTS):
                kx_copy(kind, part).start()
                ky_copy(kind, part, fresh).start()
            cache[kind] = acc[m].astype(jnp.bfloat16)

    lag = LAG
    settled = {(KEY, SUBS - 1, 1): (0, KEY), (VALUE, SUBS - 1, 1): (1, VALUE)}
    for index in range(len(kv_steps) + lag):
        take_y(steps[index])
        if index >= lag:
            step = steps[index - lag]
            take_x(step)
            if step in settled:
                settle(*settled[step])

    for step in q_steps[lag:]:
        take_y(step)

    @pl.when(grp != 0)
    def _():
        for kind, part in kv_pieces:
            kx_copy(kind, part).wait_recv()
            ky_copy(kind, part, cache).start()

    block = min(rows, 128)
    fresh_row = lax.broadcasted_iota(jnp.int32, (block, block), 0)
    fresh_col = lax.broadcasted_iota(jnp.int32, (block, block), 1)
    same = (
        lax.shift_right_logical(fresh_row, step_bits) == lax.shift_right_logical(fresh_col, step_bits)
    ) & (fresh_col <= fresh_row)
    fresh_bias = jnp.where(jnp.where(same, 1 - prompt_one, 0) == 1, 0.0, NEG)
    scale = HD ** (-0.5)

    def attend(first, head):
        span = pl.ds(pl.multiple_of(first, block), block)
        lanes = slice(head * HD, (head + 1) * HD)
        query = qbuf[span, lanes]

        def scored(keys, mask):
            return lax.dot_general(
                query, keys, contract_last, preferred_element_type=jnp.float32
            ) * scale + mask

        scores = [
            scored(cache[0, :, lanes], bias[span, 0:chip_rows]),
            scored(cache[2, :, lanes], bias[span, chip_rows : 2 * chip_rows]),
            scored(fresh[0, span, lanes], fresh_bias),
        ]
        values = [cache[1, :, lanes], cache[3, :, lanes], fresh[1, span, lanes]]
        top = jnp.maximum(
            jnp.maximum(
                jnp.max(scores[0], axis=1, keepdims=True), jnp.max(scores[1], axis=1, keepdims=True)
            ),
            jnp.max(scores[2], axis=1, keepdims=True),
        )
        total = jnp.zeros((block, 1), jnp.float32)
        summed = jnp.zeros((block, HD), jnp.float32)
        for score, value in zip(scores, values):
            weight = jnp.exp(score - top)
            total += jnp.sum(weight, axis=1, keepdims=True)
            summed += jnp.dot(weight.astype(jnp.bfloat16), value, preferred_element_type=jnp.float32)
        return (summed / total).astype(jnp.bfloat16)

    swaps_out = []
    for head in range(heads):
        lanes = slice(head * HD, (head + 1) * HD)
        for rel in range(2):
            take_x((QUERY, head, rel))
        qbuf[:, lanes] = acc[QUERY, :, lanes].astype(jnp.bfloat16)
        if head == 0:
            for kind, part in kv_pieces:
                ky_copy(kind, part, cache).wait_recv()
        for at in range(rows // block):
            osend[head, at * block : (at + 1) * block] = attend((1 - core) * rows + at * block, head)
        swap_out = remote(osend.at[head], orecv.at[head], o_send.at[head], o_recv.at[head], partner)
        swap_out.start()
        swaps_out.append(swap_out)
        for at in range(rows // block):
            own_lanes = pl.ds(pl.multiple_of(core * half + head * HD, HD), HD)
            out[at * block : (at + 1) * block, own_lanes] = attend(core * rows + at * block, head)
    for head, swap_out in enumerate(swaps_out):
        swap_out.wait()
        out[:, pl.ds(pl.multiple_of((1 - core) * half + head * HD, HD), HD)] = orecv[head]

    for copy in sent:
        copy.wait_send()

    @pl.when(grp == 0)
    def _():
        for kind, part in kv_pieces:
            kx_copy(kind, part).wait_send()
            ky_copy(kind, part, fresh).wait_send()

    @pl.when(grp != 0)
    def _():
        for kind, part in kv_pieces:
            ky_copy(kind, part, cache).wait_send()


def fused(hidden, w_query, w_key, w_value, prompt_len, page_table):
    rows, model = hidden.shape[1:]
    depth, width = w_query.shape
    half = width // 2
    chip_rows = 2 * rows
    heads = half // HD
    copies = 8 * SUBS + 4 * heads
    dma = pltpu.SemaphoreType.DMA
    anywhere = pl.BlockSpec(memory_space=pltpu.HBM)
    vmem = pl.BlockSpec(memory_space=pltpu.VMEM)
    result = pl.pallas_call(
        fused_kernel,
        out_shape=jax.ShapeDtypeStruct((rows, width), jnp.bfloat16),
        in_specs=[anywhere] * 6,
        out_specs=vmem,
        scratch_shapes=[
            pltpu.VMEM((1, prompt_len.shape[0]), jnp.int32),
            pltpu.VMEM(page_table.shape[::-1], jnp.int32),
            pltpu.VMEM((chip_rows, model), jnp.bfloat16),
            pltpu.VMEM((6, depth, half), jnp.bfloat16),
            pltpu.VMEM((8 * SUBS, depth // 2 // SUBS, half), jnp.bfloat16),
            pltpu.VMEM((4 * heads, depth // 2, HD), jnp.bfloat16),
            pltpu.VMEM((3, chip_rows, half), jnp.float32),
            pltpu.VMEM((chip_rows, half), jnp.bfloat16),
            pltpu.VMEM((2, chip_rows, half), jnp.bfloat16),
            pltpu.VMEM((4, chip_rows, half), jnp.bfloat16),
            pltpu.VMEM((chip_rows, 2 * chip_rows), jnp.float32),
            pltpu.VMEM((heads, rows, HD), jnp.bfloat16),
            pltpu.VMEM((heads, rows, HD), jnp.bfloat16),
            dma((copies,)), dma((copies,)), dma((copies,)), dma((copies,)),
            dma((4,)), dma((4,)), dma((6,)),
            dma((2 * PARTS,)), dma((2 * PARTS,)), dma((2 * PARTS,)), dma((2 * PARTS,)),
            dma((heads,)), dma((heads,)),
        ],
        compiler_params=pltpu.CompilerParams(
            collective_id=0, has_side_effects=True, vmem_limit_bytes=67043328
        ),
    )(hidden, w_query, w_key, w_value, prompt_len.reshape(1, -1), page_table.T)
    return result[None]


def solution(mesh):
    paired = mesh.shape["grp"] == 2 and mesh.shape["seq"] == 4
    return jax.shard_map(
        fused if paired else on_device,
        mesh=mesh,
        in_specs=(P("grp", "seq", None), P("seq", "tp"), P("seq", "tp"), P("seq", "tp"), P(), P()),
        out_specs=P("grp", "seq", "tp"),
        check_vma=False,
    )
```

profile of v0, /device:TPU:27, one launch (start us, length us, event | category | flops | bytes accessed | tf_op | source)
XLA Modules:
  0.0 62.3 jit_solution(6668674086821506893)
XLA Ops:
  0.0 60.6 %shard_map.64 = bf16[256,512]{1,0:T(8,128)(2,1)} custom-call(bf16[1,256,4096]{2,1,0:T(8,128)(2,1)} %hidden.1, bf16[1024,512]{1,0:T(8,128)(2,1)} %w_query.1, bf16[1024,512]{1,0:T(8,128)(2,1)} %w_key.1, bf16[1024,512]{1,0:T(8,128)(2,1)} %w_value.1, s32[1,256]{1,0:T(1,128)} %bitcast.5, s32[32,256]{1,0:T(8,128)} %bitcast.4), custom_call_target="tpu_custom_call" | custom-call | tf_op jit(solution)/shard_map/pallas_call | solution.py:459
  60.7 1.7 %copy.8 = bf16[1,256,512]{2,1,0:T(8,128)(2,1)} copy(bf16[1,256,512]{2,1,0:T(8,128)(2,1)} %bitcast.3) | data formatting | bytes 524288
where the time goes:
time: 62.5 us; the launch traced here: 62.3 us
  Pallas kernels  60.6 us (97%)
  local copies, waits for them, and re-layouts  1.67 us (3%)
    pallas_call x1, Pallas kernels, fused(): pl.pallas_call(fused_kernel, out_shape=jax.ShapeDtypeStruct((rows, width)...  60.6 us
    unnamed x1, local copies, waits for them, and re-layouts  1.67 us

commit v1 on v0

v1 whole, which is shorter than its diff:
```python
import math

import jax
import jax.numpy as jnp
from jax import lax
from jax.experimental import pallas as pl
from jax.experimental.pallas import tpu as pltpu
from jax.sharding import PartitionSpec as P

HD = 128
PAGE = 16
STEPS = 4


NEG = -1e30


def from_behind(value, axis, steps):
    count = lax.axis_size(axis)
    first, last = (max(0, -steps), min(count, count - steps))
    return lax.ppermute(value, axis, [(source, source + steps) for source in range(first, last)])


def partial_attention(query, keys, values, allowed):
    rows = query.shape[0]
    heads = query.shape[1] // HD
    query_heads = query.reshape(rows, heads, HD)
    key_heads = keys.reshape(keys.shape[0], heads, HD)
    value_heads = values.reshape(values.shape[0], heads, HD)
    scores = jnp.einsum(
        "rhd,shd->hrs", query_heads, key_heads, preferred_element_type=jnp.float32
    ) * HD ** (-0.5)
    scores = jnp.where(allowed[None], scores, NEG)
    top = jnp.max(scores, axis=2)
    weights = jnp.where(allowed[None], jnp.exp(scores - top[:, :, None]), 0.0)
    total = jnp.sum(weights, axis=2)
    summed = jnp.einsum(
        "hrs,shd->rhd",
        weights.astype(jnp.bfloat16),
        value_heads,
        preferred_element_type=jnp.float32,
    )
    return (top, total, summed.reshape(rows, heads * HD))


def rescale(summed, factor):
    rows = summed.shape[0]
    heads = factor.shape[0]
    return (summed.reshape(rows, heads, HD) * factor.T[:, :, None]).reshape(rows, heads * HD)


def combine(first, second):
    top = jnp.maximum(first[0], second[0])
    early = jnp.exp(first[0] - top)
    later = jnp.exp(second[0] - top)
    return (
        top,
        first[1] * early + second[1] * later,
        rescale(first[2], early) + rescale(second[2], later),
    )


def finish(state):
    return rescale(state[2], 1.0 / state[1]).astype(jnp.bfloat16)


def row_mask(tables, lengths, key_pos):
    pages = key_pos // PAGE
    member = jnp.any(tables[:, :, None] == pages[None, None, :], axis=1)
    allowed = member & (key_pos[None, :] < lengths[:, None])
    return jnp.repeat(allowed, STEPS, axis=0)


def blocked(carry, keys, values, query, mask_of):
    count = keys.shape[0]
    block = math.gcd(count, 512)

    def one_block(state, offset):
        piece_keys = lax.dynamic_slice_in_dim(keys, offset, block, 0)
        piece_values = lax.dynamic_slice_in_dim(values, offset, block, 0)
        key_pos = offset + jnp.arange(block)
        return (
            combine(state, partial_attention(query, piece_keys, piece_values, mask_of(key_pos))),
            None,
        )

    offsets = jnp.arange(count // block) * block
    state, unused = lax.scan(one_block, carry, offsets)
    return state


def on_device(hidden, w_query, w_key, w_value, prompt_len, page_table):
    local = hidden[0]
    rows = local.shape[0]
    width = w_query.shape[1]
    heads = width // HD
    seq_index = lax.axis_index("seq")
    is_prompt = lax.axis_index("grp") == 0
    empty = jnp.zeros((rows, width), jnp.float32)
    piece = (
        lax.all_gather(w_query, "seq", axis=0, tiled=True),
        lax.all_gather(w_key, "seq", axis=0, tiled=True),
        lax.all_gather(w_value, "seq", axis=0, tiled=True),
    )
    projected = tuple(
        (jnp.dot(local, weight, preferred_element_type=jnp.float32) for weight in piece)
    )
    query, keys, values = [item.astype(jnp.bfloat16) for item in projected]
    positions = seq_index * rows + jnp.arange(rows)
    start_state = (
        jnp.full((heads, rows), NEG, jnp.float32),
        jnp.zeros((heads, rows), jnp.float32),
        empty,
    )
    given_keys, given_values = from_behind((keys, values), "grp", 1)
    cache_keys = jnp.where(is_prompt, keys, given_keys)
    cache_values = jnp.where(is_prompt, values, given_values)
    row_count = rows // STEPS
    own_tables = lax.dynamic_slice_in_dim(page_table, seq_index * row_count, row_count, 0)
    own_lengths = lax.dynamic_slice_in_dim(prompt_len, seq_index * row_count, row_count, 0)

    def mask_of(key_pos):
        causal = key_pos[None, :] <= positions[:, None]
        listed = row_mask(own_tables, own_lengths, key_pos)
        return jnp.where(is_prompt, causal, listed)

    piece = (
        lax.all_gather(cache_keys, "seq", axis=0, tiled=True),
        lax.all_gather(cache_values, "seq", axis=0, tiled=True),
    )
    state = blocked(start_state, piece[0], piece[1], query, mask_of)
    frame_row = positions // STEPS
    own_rows = (frame_row[:, None] == frame_row[None, :]) & (
        positions[None, :] <= positions[:, None]
    )
    fresh = partial_attention(query, keys, values, own_rows)
    prefill_out = finish(state)
    decode_out = finish(combine(state, fresh))
    return jnp.where(is_prompt, prefill_out, decode_out)[None]


QUERY, KEY, VALUE = 0, 1, 2
PROMPT, DECODE = 0, 1
CHUNKS = 8
KV_PIECES = 2


def fused_kernel(
    hidden, w_query, w_key, w_value, lengths_in, tables_in, out,
    lengths, tables, states, kv_weights, q_weights, kv_acc, q_acc, own_kv, far_kv, qbuf,
    near_bias, far_bias, near_scores, fresh_scores, far_part, near_part, totals, osend, orecv,
    local_sem, d_send, d_recv, y_send, y_recv, hd_send, hd_recv, hx_send, hx_recv, hz_send, hz_recv,
    hp_send, hp_recv, k_send, k_recv, o_send, o_recv,
):
    inputs = {QUERY: w_query, KEY: w_key, VALUE: w_value}
    order = (KEY, VALUE, QUERY)
    rows = hidden.shape[1]
    depth = w_query.shape[0]
    half_rows = rows // 2
    chunk = half_rows // CHUNKS
    chip_rows = 2 * rows
    block = rows // 2
    blocks = chip_rows // block
    grp = lax.axis_index("grp")
    seq = lax.axis_index("seq")
    tp = lax.axis_index("tp")
    y = seq // 2
    core = seq % 2
    side = tp % 2
    partner = {"seq": 2 * y + 1 - core}
    across = [{"seq": 2 * (1 - y) + core}, {"seq": 2 * (1 - y) + 1 - core}]
    beside = [{"grp": 1 - grp, "seq": 2 * y + core}, {"grp": 1 - grp, "seq": 2 * y + 1 - core}]
    above = {"tp": tp + 1 - 2 * side}
    cores = [core, 1 - core]

    def remote(src, dst, send, recv, to):
        return pltpu.make_async_remote_copy(
            src_ref=src, dst_ref=dst, send_sem=send, recv_sem=recv,
            device_id=to, device_id_type=pl.DeviceIdType.MESH,
        )

    def head_lanes(of_grp, of_core):
        return pl.ds(pl.multiple_of((2 * of_grp + of_core) * HD, HD), HD)

    def quarter(of_seq):
        return pl.ds(pl.multiple_of(of_seq * depth, depth), depth)

    def landing(m, of_seq):
        if m == QUERY:
            return q_weights.at[quarter(of_seq)]
        return kv_weights.at[quarter(of_seq), (m - KEY) * HD : (m - KEY + 1) * HD]

    keeps = {
        m: pltpu.make_async_copy(inputs[m].at[:, head_lanes(grp, core)], landing(m, seq), local_sem.at[m])
        for m in order
    }
    table_keep = pltpu.make_async_copy(tables_in, tables, local_sem.at[3])
    length_keep = pltpu.make_async_copy(lengths_in, lengths, local_sem.at[4])
    my_rows = pl.ds(pl.multiple_of(core * rows, rows), rows)
    own_keep = pltpu.make_async_copy(hidden.at[0], states.at[grp, my_rows], local_sem.at[5])
    table_keep.start()
    length_keep.start()
    own_keep.start()
    for m in order:
        keeps[m].start()

    barrier = pltpu.get_barrier_semaphore()
    for peer in (partner, *across, *beside, above):
        pl.semaphore_signal(barrier, inc=1, device_id=peer, device_id_type=pl.DeviceIdType.MESH)
    pl.semaphore_wait(barrier, 6)

    sent = []

    def launch(copy):
        copy.start()
        sent.append(copy)

    def y_weight(m, rel):
        at = m * 2 + rel
        return remote(
            inputs[m].at[:, head_lanes(grp, cores[rel])], landing(m, seq), y_send.at[at], y_recv.at[at], across[rel]
        )

    def y_arrival(m, rel):
        at = m * 2 + rel
        spot = landing(m, 2 * (1 - y) + cores[rel])
        return remote(spot, spot, y_send.at[at], y_recv.at[at], across[rel])

    def chunk_rows(which, of_core, at):
        return pl.ds(pl.multiple_of(of_core * rows + which * half_rows + at * chunk, chunk), chunk)

    def x_chunk(at):
        source = pl.ds(pl.multiple_of(side * half_rows + at * chunk, chunk), chunk)
        return remote(
            hidden.at[0, source], states.at[grp, chunk_rows(side, core, at)],
            hx_send.at[at], hx_recv.at[at], beside[0],
        )

    def x_arrival(at):
        spot = states.at[1 - grp, chunk_rows(side, core, at)]
        return remote(spot, spot, hx_send.at[at], hx_recv.at[at], beside[0])

    def z_chunk(at):
        spot = states.at[1 - grp, chunk_rows(side, core, at)]
        return remote(spot, spot, hz_send.at[at], hz_recv.at[at], above)

    def z_arrival(at):
        spot = states.at[1 - grp, chunk_rows(1 - side, core, at)]
        return remote(spot, spot, hz_send.at[at], hz_recv.at[at], above)

    def relay_chunk(which, at, of_core):
        spot = states.at[1 - grp, chunk_rows(side if which == 0 else 1 - side, of_core, at)]
        number = which * CHUNKS + at
        return remote(spot, spot, hp_send.at[number], hp_recv.at[number], partner)

    for m in order:
        for rel in range(2):
            launch(y_weight(m, rel))
    for at in range(CHUNKS):
        launch(x_chunk(at))
    d_weights = {
        m: remote(inputs[m].at[:, head_lanes(grp, 1 - core)], landing(m, seq), d_send.at[m], d_recv.at[m], partner)
        for m in order
    }
    own_swap = remote(hidden.at[0], states.at[grp, my_rows], hd_send, hd_recv, partner)
    launch(d_weights[KEY])
    launch(d_weights[VALUE])
    launch(own_swap)
    launch(d_weights[QUERY])

    table_keep.wait()
    length_keep.wait()
    decode_rows = chip_rows // STEPS
    pages = 2 * chip_rows // PAGE
    own_rows = pl.ds(pl.multiple_of(y * decode_rows, decode_rows), decode_rows)
    own_table = tables[:, own_rows]
    own_length = lengths[:, own_rows]
    page_row = lax.broadcasted_iota(jnp.int32, (pages, decode_rows), 0)
    member = own_table[0:1, :] == page_row
    for listed in range(1, own_table.shape[0]):
        member = member | (own_table[listed : listed + 1, :] == page_row)
    member = jnp.where(member, 1.0, 0.0).astype(jnp.bfloat16)
    step_bits = STEPS.bit_length() - 1
    page_bits = PAGE.bit_length() - 1
    spread = (
        lax.shift_right_logical(lax.broadcasted_iota(jnp.int32, (chip_rows, decode_rows), 0), step_bits)
        == lax.broadcasted_iota(jnp.int32, (chip_rows, decode_rows), 1)
    )
    spread = jnp.where(spread, 1.0, 0.0).astype(jnp.bfloat16)
    contract_last = (((1,), (1,)), ((), ()))
    for which, bias in enumerate((near_bias, far_bias)):
        base = (y if which == 0 else 1 - y) * chip_rows
        key_page = lax.shift_right_logical(
            lax.broadcasted_iota(jnp.int32, (chip_rows, pages), 0) + base, page_bits
        )
        unfold = lax.broadcasted_iota(jnp.int32, (chip_rows, pages), 1) == key_page
        unfold = jnp.where(unfold, 1.0, 0.0).astype(jnp.bfloat16)
        seen = jnp.dot(unfold, member, preferred_element_type=jnp.float32)
        key_pos = lax.broadcasted_iota(jnp.int32, (chip_rows, decode_rows), 0) + base
        seen = jnp.where(key_pos < own_length, seen, 0.0).astype(jnp.bfloat16)
        listed = lax.dot_general(spread, seen, contract_last, preferred_element_type=jnp.float32)
        bias[...] = jnp.where(listed > 0.5, 0.0, NEG)

    def kv_dot(group, of_seq):
        return jnp.dot(
            states[group, :, quarter(of_seq)], kv_weights[quarter(of_seq), :], preferred_element_type=jnp.float32
        )

    def q_dot(group, of_seq):
        return jnp.dot(
            states[group, :, quarter(of_seq)], q_weights[quarter(of_seq), :], preferred_element_type=jnp.float32
        )

    near_seqs = [seq, 2 * y + 1 - core]
    far_seqs = [2 * (1 - y) + core, 2 * (1 - y) + 1 - core]

    def take_x(at):
        x_arrival(at).wait_recv()
        launch(z_chunk(at))
        launch(relay_chunk(0, at, core))

    def take_z(at):
        z_arrival(at).wait_recv()
        launch(relay_chunk(1, at, core))

    def near_kv():
        own_keep.wait()
        own_swap.wait_recv()
        for m in (KEY, VALUE):
            keeps[m].wait()
            d_weights[m].wait_recv()
        kv_acc[grp] = kv_dot(grp, near_seqs[0]) + kv_dot(grp, near_seqs[1])

    def near_q():
        keeps[QUERY].wait()
        d_weights[QUERY].wait_recv()
        q_acc[grp] = q_dot(grp, near_seqs[0]) + q_dot(grp, near_seqs[1])

    def far_kv_dot(rel):
        for m in (KEY, VALUE):
            y_arrival(m, rel).wait_recv()
        kv_acc[grp] += kv_dot(grp, far_seqs[rel])

    LATE = 2
    for at in range(CHUNKS + LATE):
        if at < CHUNKS:
            take_x(at)
        if at >= LATE:
            take_z(at - LATE)
        if at == 0:
            near_kv()
        if at == 1:
            near_q()
    for rel in range(2):
        far_kv_dot(rel)
    for which in range(2):
        for at in range(CHUNKS):
            relay_chunk(which, at, 1 - core).wait_recv()
    other = 1 - grp
    kv_acc[other] = (kv_dot(other, near_seqs[0]) + kv_dot(other, near_seqs[1])) + (
        kv_dot(other, far_seqs[0]) + kv_dot(other, far_seqs[1])
    )
    for group in (PROMPT, DECODE):
        for kind in range(2):
            own_kv[group, kind] = kv_acc[group, :, kind * HD : (kind + 1) * HD].astype(jnp.bfloat16)

    def kv_copy(kind, piece):
        span = pl.ds(piece * (chip_rows // KV_PIECES), chip_rows // KV_PIECES)
        at = kind * KV_PIECES + piece
        return remote(
            own_kv.at[PROMPT, kind, span], far_kv.at[kind, span], k_send.at[at], k_recv.at[at], across[0]
        )

    for kind in range(2):
        for piece in range(KV_PIECES):
            launch(kv_copy(kind, piece))
    q_acc[other] = q_dot(other, near_seqs[0]) + q_dot(other, near_seqs[1])
    for rel in range(2):
        y_arrival(QUERY, rel).wait_recv()
        if rel == 0:
            for group in (PROMPT, DECODE):
                q_acc[group] += q_dot(group, far_seqs[rel])
        else:
            for group in (PROMPT, DECODE):
                qbuf[group] = (q_acc[group] + q_dot(group, far_seqs[rel])).astype(jnp.bfloat16)

    scale = HD ** (-0.5)
    fresh_row = lax.broadcasted_iota(jnp.int32, (block, block), 0)
    fresh_col = lax.broadcasted_iota(jnp.int32, (block, block), 1)
    same = (
        lax.shift_right_logical(fresh_row, step_bits) == lax.shift_right_logical(fresh_col, step_bits)
    ) & (fresh_col <= fresh_row)
    fresh_bias = jnp.where(same, 0.0, NEG)
    far_prompt_bias = jnp.where(y == 1, 0.0, NEG)

    def product(group, span, keys):
        return lax.dot_general(
            qbuf[group, span], keys, contract_last, preferred_element_type=jnp.float32
        ) * scale

    for at in range(blocks):
        span = slice(at * block, (at + 1) * block)
        causal = (
            lax.broadcasted_iota(jnp.int32, (block, chip_rows), 1)
            <= lax.broadcasted_iota(jnp.int32, (block, chip_rows), 0) + at * block
        )
        near_scores[PROMPT, span] = jnp.where(causal, product(PROMPT, span, own_kv[PROMPT, 0]), NEG)
        near_scores[DECODE, span] = product(DECODE, span, own_kv[PROMPT, 0]) + near_bias[span]
        fresh_scores[span] = product(DECODE, span, own_kv[DECODE, 0, span]) + fresh_bias

    for piece in range(KV_PIECES):
        kv_copy(0, piece).wait_recv()

    def weigh(group, at):
        span = slice(at * block, (at + 1) * block)
        far_score = product(group, span, far_kv[0])
        far_score = far_score + (far_prompt_bias if group == PROMPT else far_bias[span])
        near_score = near_scores[group, span]
        top = jnp.maximum(jnp.max(near_score, axis=1, keepdims=True), jnp.max(far_score, axis=1, keepdims=True))
        if group == DECODE:
            top = jnp.maximum(top, jnp.max(fresh_scores[span], axis=1, keepdims=True))
        near = jnp.exp(near_score - top)
        far = jnp.exp(far_score - top)
        total = jnp.sum(near, axis=1, keepdims=True) + jnp.sum(far, axis=1, keepdims=True)
        summed = jnp.dot(near.astype(jnp.bfloat16), own_kv[PROMPT, 1], preferred_element_type=jnp.float32)
        if group == DECODE:
            fresh = jnp.exp(fresh_scores[span] - top)
            total += jnp.sum(fresh, axis=1, keepdims=True)
            summed += jnp.dot(
                fresh.astype(jnp.bfloat16), own_kv[DECODE, 1, span], preferred_element_type=jnp.float32
            )
        far_part[group, span] = far.astype(jnp.bfloat16)
        near_part[group, span] = summed
        totals[group, span] = jnp.broadcast_to(total, (block, HD))

    for at in range(blocks):
        for group in (PROMPT, DECODE):
            weigh(group, at)
    for piece in range(KV_PIECES):
        kv_copy(1, piece).wait_recv()

    def attended(group, of_core, at):
        span = pl.ds(pl.multiple_of(of_core * rows + at * block, block), block)
        summed = near_part[group, span] + jnp.dot(
            far_part[group, span], far_kv[1], preferred_element_type=jnp.float32
        )
        return (summed / totals[group, span]).astype(jnp.bfloat16)

    pieces = rows // block

    def out_copy(source, at):
        number = source * pieces + at
        span = pl.ds(at * block, block)
        to = (partner, beside[0], beside[1])[source]
        return remote(
            osend.at[source, span], orecv.at[source, span], o_send.at[number], o_recv.at[number], to
        )

    for source in (2, 1):
        for at in range(pieces):
            osend[source, at * block : (at + 1) * block] = attended(other, cores[source - 1], at)
            launch(out_copy(source, at))
    for at in range(pieces):
        osend[0, at * block : (at + 1) * block] = attended(grp, 1 - core, at)
        launch(out_copy(0, at))
    for at in range(pieces):
        out[at * block : (at + 1) * block, head_lanes(grp, core)] = attended(grp, core, at)
    for source in (0, 2, 1):
        lanes = (head_lanes(grp, 1 - core), head_lanes(other, core), head_lanes(other, 1 - core))[source]
        for at in range(pieces):
            out_copy(source, at).wait_recv()
            out[at * block : (at + 1) * block, lanes] = orecv[source, at * block : (at + 1) * block]

    for copy in sent:
        copy.wait_send()


def fused(hidden, w_query, w_key, w_value, prompt_len, page_table):
    rows, model = hidden.shape[1:]
    depth, width = w_query.shape
    chip_rows = 2 * rows
    block = rows // 2
    dma = pltpu.SemaphoreType.DMA
    anywhere = pl.BlockSpec(memory_space=pltpu.HBM)
    vmem = pl.BlockSpec(memory_space=pltpu.VMEM)
    pieces = rows // block
    result = pl.pallas_call(
        fused_kernel,
        out_shape=jax.ShapeDtypeStruct((rows, width), jnp.bfloat16),
        in_specs=[anywhere] * 6,
        out_specs=vmem,
        scratch_shapes=[
            pltpu.VMEM((1, prompt_len.shape[0]), jnp.int32),
            pltpu.VMEM(page_table.shape[::-1], jnp.int32),
            pltpu.VMEM((2, chip_rows, model), jnp.bfloat16),
            pltpu.VMEM((model, 2 * HD), jnp.bfloat16),
            pltpu.VMEM((model, HD), jnp.bfloat16),
            pltpu.VMEM((2, chip_rows, 2 * HD), jnp.float32),
            pltpu.VMEM((2, chip_rows, HD), jnp.float32),
            pltpu.VMEM((2, 2, chip_rows, HD), jnp.bfloat16),
            pltpu.VMEM((2, chip_rows, HD), jnp.bfloat16),
            pltpu.VMEM((2, chip_rows, HD), jnp.bfloat16),
            pltpu.VMEM((chip_rows, chip_rows), jnp.float32),
            pltpu.VMEM((chip_rows, chip_rows), jnp.float32),
            pltpu.VMEM((2, chip_rows, chip_rows), jnp.float32),
            pltpu.VMEM((chip_rows, block), jnp.float32),
            pltpu.VMEM((2, chip_rows, chip_rows), jnp.bfloat16),
            pltpu.VMEM((2, chip_rows, HD), jnp.float32),
            pltpu.VMEM((2, chip_rows, HD), jnp.float32),
            pltpu.VMEM((3, rows, HD), jnp.bfloat16),
            pltpu.VMEM((3, rows, HD), jnp.bfloat16),
            dma((6,)), dma((3,)), dma((3,)), dma((6,)), dma((6,)), dma(()), dma(()),
            dma((CHUNKS,)), dma((CHUNKS,)), dma((CHUNKS,)), dma((CHUNKS,)),
            dma((2 * CHUNKS,)), dma((2 * CHUNKS,)),
            dma((2 * KV_PIECES,)), dma((2 * KV_PIECES,)),
            dma((3 * pieces,)), dma((3 * pieces,)),
        ],
        compiler_params=pltpu.CompilerParams(
            collective_id=0, has_side_effects=True, vmem_limit_bytes=67043328
        ),
    )(hidden, w_query, w_key, w_value, prompt_len.reshape(1, -1), page_table.T)
    return result[None]


def solution(mesh):
    paired = mesh.shape["grp"] == 2 and mesh.shape["seq"] == 4 and mesh.shape["tp"] % 2 == 0
    return jax.shard_map(
        fused if paired else on_device,
        mesh=mesh,
        in_specs=(P("grp", "seq", None), P("seq", "tp"), P("seq", "tp"), P("seq", "tp"), P(), P()),
        out_specs=P("grp", "seq", "tp"),
        check_vma=False,
    )
```

time: 62.5 us -> 53.1 us (0.85)
  the two profiles are of different devices: /device:TPU:27 before, /device:TPU:0 now
where the time goes in v1:
time: 53.1 us; the launch traced here: 52.9 us
  Pallas kernels  51.2 us (96%)
  local copies, waits for them, and re-layouts  1.67 us (3%)
    pallas_call x1, Pallas kernels, fused(): pl.pallas_call(fused_kernel, out_shape=jax.ShapeDtypeStruct((rows, width)...  51.2 us
    unnamed x1, local copies, waits for them, and re-layouts  1.67 us

profile of v1, /device:TPU:0, one launch (start us, length us, event | category | flops | bytes accessed | tf_op | source)
XLA Modules:
  0.0 52.9 jit_solution(4333399159600341284)
XLA Ops:
  0.0 51.2 %shard_map.64 = bf16[256,512]{1,0:T(8,128)(2,1)} custom-call(bf16[1,256,4096]{2,1,0:T(8,128)(2,1)} %hidden.1, bf16[1024,512]{1,0:T(8,128)(2,1)} %w_query.1, bf16[1024,512]{1,0:T(8,128)(2,1)} %w_key.1, bf16[1024,512]{1,0:T(8,128)(2,1)} %w_value.1, s32[1,256]{1,0:T(1,128)} %bitcast.5, s32[32,256]{1,0:T(8,128)} %bitcast.4), custom_call_target="tpu_custom_call" | custom-call | tf_op jit(solution)/shard_map/pallas_call | solution.py:487
  51.2 1.7 %copy.8 = bf16[1,256,512]{2,1,0:T(8,128)(2,1)} copy(bf16[1,256,512]{2,1,0:T(8,128)(2,1)} %bitcast.3) | data formatting | bytes 524288

commit v2 on v0

v2 whole, which is shorter than its diff:
```python
import functools
import math

import jax
import jax.numpy as jnp
from jax import lax
from jax.experimental import pallas as pl
from jax.experimental.pallas import tpu as pltpu
from jax.sharding import PartitionSpec as P

HD = 128
PAGE = 16
STEPS = 4


NEG = -1e30


def from_behind(value, axis, steps):
    count = lax.axis_size(axis)
    first, last = (max(0, -steps), min(count, count - steps))
    return lax.ppermute(value, axis, [(source, source + steps) for source in range(first, last)])


def partial_attention(query, keys, values, allowed):
    rows = query.shape[0]
    heads = query.shape[1] // HD
    query_heads = query.reshape(rows, heads, HD)
    key_heads = keys.reshape(keys.shape[0], heads, HD)
    value_heads = values.reshape(values.shape[0], heads, HD)
    scores = jnp.einsum(
        "rhd,shd->hrs", query_heads, key_heads, preferred_element_type=jnp.float32
    ) * HD ** (-0.5)
    scores = jnp.where(allowed[None], scores, NEG)
    top = jnp.max(scores, axis=2)
    weights = jnp.where(allowed[None], jnp.exp(scores - top[:, :, None]), 0.0)
    total = jnp.sum(weights, axis=2)
    summed = jnp.einsum(
        "hrs,shd->rhd",
        weights.astype(jnp.bfloat16),
        value_heads,
        preferred_element_type=jnp.float32,
    )
    return (top, total, summed.reshape(rows, heads * HD))


def rescale(summed, factor):
    rows = summed.shape[0]
    heads = factor.shape[0]
    return (summed.reshape(rows, heads, HD) * factor.T[:, :, None]).reshape(rows, heads * HD)


def combine(first, second):
    top = jnp.maximum(first[0], second[0])
    early = jnp.exp(first[0] - top)
    later = jnp.exp(second[0] - top)
    return (
        top,
        first[1] * early + second[1] * later,
        rescale(first[2], early) + rescale(second[2], later),
    )


def finish(state):
    return rescale(state[2], 1.0 / state[1]).astype(jnp.bfloat16)


def row_mask(tables, lengths, key_pos):
    pages = key_pos // PAGE
    member = jnp.any(tables[:, :, None] == pages[None, None, :], axis=1)
    allowed = member & (key_pos[None, :] < lengths[:, None])
    return jnp.repeat(allowed, STEPS, axis=0)


def blocked(carry, keys, values, query, mask_of):
    count = keys.shape[0]
    block = math.gcd(count, 512)

    def one_block(state, offset):
        piece_keys = lax.dynamic_slice_in_dim(keys, offset, block, 0)
        piece_values = lax.dynamic_slice_in_dim(values, offset, block, 0)
        key_pos = offset + jnp.arange(block)
        return (
            combine(state, partial_attention(query, piece_keys, piece_values, mask_of(key_pos))),
            None,
        )

    offsets = jnp.arange(count // block) * block
    state, unused = lax.scan(one_block, carry, offsets)
    return state


def on_device(hidden, w_query, w_key, w_value, prompt_len, page_table):
    local = hidden[0]
    rows = local.shape[0]
    width = w_query.shape[1]
    heads = width // HD
    seq_index = lax.axis_index("seq")
    is_prompt = lax.axis_index("grp") == 0
    empty = jnp.zeros((rows, width), jnp.float32)
    piece = (
        lax.all_gather(w_query, "seq", axis=0, tiled=True),
        lax.all_gather(w_key, "seq", axis=0, tiled=True),
        lax.all_gather(w_value, "seq", axis=0, tiled=True),
    )
    projected = tuple(
        (jnp.dot(local, weight, preferred_element_type=jnp.float32) for weight in piece)
    )
    query, keys, values = [item.astype(jnp.bfloat16) for item in projected]
    positions = seq_index * rows + jnp.arange(rows)
    start_state = (
        jnp.full((heads, rows), NEG, jnp.float32),
        jnp.zeros((heads, rows), jnp.float32),
        empty,
    )
    given_keys, given_values = from_behind((keys, values), "grp", 1)
    cache_keys = jnp.where(is_prompt, keys, given_keys)
    cache_values = jnp.where(is_prompt, values, given_values)
    row_count = rows // STEPS
    own_tables = lax.dynamic_slice_in_dim(page_table, seq_index * row_count, row_count, 0)
    own_lengths = lax.dynamic_slice_in_dim(prompt_len, seq_index * row_count, row_count, 0)

    def mask_of(key_pos):
        causal = key_pos[None, :] <= positions[:, None]
        listed = row_mask(own_tables, own_lengths, key_pos)
        return jnp.where(is_prompt, causal, listed)

    piece = (
        lax.all_gather(cache_keys, "seq", axis=0, tiled=True),
        lax.all_gather(cache_values, "seq", axis=0, tiled=True),
    )
    state = blocked(start_state, piece[0], piece[1], query, mask_of)
    frame_row = positions // STEPS
    own_rows = (frame_row[:, None] == frame_row[None, :]) & (
        positions[None, :] <= positions[:, None]
    )
    fresh = partial_attention(query, keys, values, own_rows)
    prefill_out = finish(state)
    decode_out = finish(combine(state, fresh))
    return jnp.where(is_prompt, prefill_out, decode_out)[None]


QUERY, KEY, VALUE = 0, 1, 2
OWN, OTHER = 0, 1
SUBS = 2


def fused_kernel(
    planes, hidden, w_query, w_key, w_value, lengths_in, tables_in, out,
    lengths, tables, own, other, weights, acc, wide_out, wide_in, value_out, value_in, qbuf, fresh, cache, bias, osend, orecv,
    local_sem, w_send, w_recv, hy_send, hy_recv, up_send, down_send, hz_recv, p_send, p_recv,
    kx_send, kx_recv, kd_send, kd_recv, o_send, o_recv,
):
    inputs = {QUERY: w_query, KEY: w_key, VALUE: w_value}
    rows = hidden.shape[1]
    depth, width = w_query.shape
    span = 2 * depth
    half = width // 2
    heads = half // HD
    block = rows // 2
    chunk = rows // planes // SUBS
    grp = lax.axis_index("grp")
    seq = lax.axis_index("seq")
    tp = lax.axis_index("tp")
    y = seq // 2
    core = seq % 2
    side = tp // (planes // 2)
    partner = {"seq": 2 * y + 1 - core}
    across = {"seq": 2 * (1 - y) + core}
    beside = {"grp": 1 - grp}
    above = {"tp": lax.rem(tp + 1, planes)}
    below = {"tp": lax.rem(tp + planes - 1, planes)}
    kinds = {KEY: 0, VALUE: 1}
    seqs = [2 * y + core, 2 * (1 - y) + core]
    my_heads = pl.ds(pl.multiple_of(y * half, half), half)
    their_heads = pl.ds(pl.multiple_of((1 - y) * half, half), half)
    halves = [pl.ds(pl.multiple_of(at * block, block), block) for at in (side, 1 - side)]

    def remote(src, dst, send, recv, to):
        return pltpu.make_async_remote_copy(
            src_ref=src, dst_ref=dst, send_sem=send, recv_sem=recv,
            device_id=to, device_id_type=pl.DeviceIdType.MESH,
        )

    my_depth = pl.ds(pl.multiple_of(core * depth, depth), depth)
    keeps = {m: pltpu.make_async_copy(inputs[m], weights.at[m, my_depth], local_sem.at[m]) for m in inputs}
    table_keep = pltpu.make_async_copy(tables_in, tables, local_sem.at[3])
    length_keep = pltpu.make_async_copy(lengths_in, lengths, local_sem.at[4])
    own_keep = pltpu.make_async_copy(
        hidden.at[0, :, pl.ds(pl.multiple_of(y * span, span), span)], own, local_sem.at[5]
    )
    table_keep.start()
    length_keep.start()
    own_keep.start()
    for m in (KEY, VALUE, QUERY):
        keeps[m].start()

    barrier = pltpu.get_barrier_semaphore()
    for peer in (across, partner, beside):
        pl.semaphore_signal(barrier, inc=1, device_id=peer, device_id_type=pl.DeviceIdType.MESH)

    @pl.when(tp < planes - 1)
    def _():
        pl.semaphore_signal(barrier, inc=1, device_id=above, device_id_type=pl.DeviceIdType.MESH)

    @pl.when(tp > 0)
    def _():
        pl.semaphore_signal(barrier, inc=1, device_id=below, device_id_type=pl.DeviceIdType.MESH)

    ends = jnp.where(tp == 0, 1, 0) + jnp.where(tp == planes - 1, 1, 0)
    pl.semaphore_wait(barrier, 5 - ends)

    def chunk_rows(plane, sub):
        return pl.ds(pl.multiple_of((plane * SUBS + sub) * chunk, chunk), chunk)

    def y_chunk(sub):
        take = chunk_rows(tp, sub)
        return remote(
            hidden.at[0, take, pl.ds(pl.multiple_of((1 - y) * span, span), span)], other.at[take],
            hy_send.at[sub], hy_recv.at[sub], across,
        )

    def z_chunk(plane, sub, up):
        take = chunk_rows(plane, sub)
        at = plane * SUBS + sub
        return remote(
            other.at[take], other.at[take], (up_send if up else down_send).at[at], hz_recv.at[at],
            above if up else below,
        )

    sent = []

    def launch(copy):
        copy.start()
        sent.append(copy)

    for sub in range(SUBS):
        launch(y_chunk(sub))
    swaps = {
        m: remote(inputs[m], weights.at[m, my_depth], w_send.at[m], w_recv.at[m], partner) for m in inputs
    }
    for m in (KEY, VALUE, QUERY):
        launch(swaps[m])

    table_keep.wait()
    length_keep.wait()
    total_rows = tables.shape[1]
    keys = cache.shape[1]
    pages = keys // PAGE
    decode_rows = rows // STEPS
    step_bits = STEPS.bit_length() - 1
    page_bits = PAGE.bit_length() - 1
    prompt_one = jnp.where(grp == 0, 1, 0)
    contract_last = (((1,), (1,)), ((), ()))
    table = tables[...]
    page_row = lax.broadcasted_iota(jnp.int32, (pages, total_rows), 0)
    member = table[0:1, :] == page_row
    for listed in range(1, table.shape[0]):
        member = member | (table[listed : listed + 1, :] == page_row)
    member = jnp.where(member, 1.0, 0.0).astype(jnp.bfloat16)
    unfold = lax.broadcasted_iota(jnp.int32, (keys, pages), 1) == lax.shift_right_logical(
        lax.broadcasted_iota(jnp.int32, (keys, pages), 0), page_bits
    )
    unfold = jnp.where(unfold, 1.0, 0.0).astype(jnp.bfloat16)
    seen = jnp.dot(unfold, member, preferred_element_type=jnp.float32)
    key_pos = lax.broadcasted_iota(jnp.int32, (keys, total_rows), 0)
    seen = jnp.where(key_pos < lengths[...], seen, 0.0).astype(jnp.bfloat16)
    for s in (OWN, OTHER):
        spread = (
            lax.shift_right_logical(lax.broadcasted_iota(jnp.int32, (rows, total_rows), 0), step_bits)
            + seqs[s] * decode_rows
            == lax.broadcasted_iota(jnp.int32, (rows, total_rows), 1)
        )
        spread = jnp.where(spread, 1.0, 0.0).astype(jnp.bfloat16)
        listed = lax.dot_general(spread, seen, contract_last, preferred_element_type=jnp.float32)
        causal = (
            lax.broadcasted_iota(jnp.int32, (rows, keys), 1)
            <= lax.broadcasted_iota(jnp.int32, (rows, keys), 0) + seqs[s] * rows
        )
        allowed = jnp.where(prompt_one == 1, jnp.where(causal, 1.0, 0.0), listed)
        bias[s] = jnp.where(allowed > 0.5, 0.0, NEG)

    def project(source, at, m, lanes):
        return jnp.dot(source[at, :], weights[m, :, lanes], preferred_element_type=jnp.float32)

    def part_at(wide, narrow, s, m, at):
        return narrow.at[s, at] if m == VALUE else wide.at[s, m, at]

    def send(source, s, at, m):
        spot = part_at(wide_out, value_out, s, m, at)
        spot[...] = project(source, at, m, their_heads).astype(spot.dtype)

    def keep(source, s, at, m):
        acc[s, m, at] = project(source, at, m, my_heads)

    def both(source, s, at, m):
        send(source, s, at, m)
        keep(source, s, at, m)

    def partial(s, m, piece):
        at = halves[piece]
        number = (s * 3 + m) * 2 + piece
        return remote(
            part_at(wide_out, value_out, s, m, at), part_at(wide_in, value_in, 1 - s, m, at),
            p_send.at[number], p_recv.at[number], across,
        )

    everything = pl.ds(0, rows)

    def pass_on(plane, sub, up, down):
        if up:

            @pl.when(tp < planes - 1)
            def _():
                z_chunk(plane, sub, True).start()

        if down:

            @pl.when(tp > 0)
            def _():
                z_chunk(plane, sub, False).start()

    def take_y(sub):
        y_chunk(sub).wait_recv()
        pass_on(tp, sub, True, True)

    def take_z(far):
        for sub in range(SUBS):

            @pl.when(tp + far < planes)
            def _():
                z_chunk(tp + far, sub, False).wait_recv()
                pass_on(tp + far, sub, False, True)

            @pl.when(tp >= far)
            def _():
                z_chunk(tp - far, sub, True).wait_recv()
                pass_on(tp - far, sub, True, False)

    own_keep.wait()
    for at, m in enumerate((KEY, VALUE, QUERY)):
        keeps[m].wait()
        swaps[m].wait_recv()
        if at < SUBS:
            take_y(at)
        for piece in range(2):
            send(own, OWN, halves[piece], m)
            launch(partial(OWN, m, piece))
        keep(own, OWN, everything, m)
    for sub in range(3, SUBS):
        take_y(sub)

    def arrived(s, m, piece):
        at = halves[piece]
        remote(
            part_at(wide_out, value_out, s, m, at), part_at(wide_in, value_in, s, m, at),
            p_send.at[((1 - s) * 3 + m) * 2 + piece], p_recv.at[((1 - s) * 3 + m) * 2 + piece], across,
        ).wait_recv()

    def settled(s, m, piece):
        at = halves[piece]
        far = part_at(wide_in, value_in, s, m, at)[...]
        return (acc[s, m, at] + far.astype(jnp.float32)).astype(jnp.bfloat16)

    def place(s, piece, of_core):
        which = side if piece == 0 else 1 - side
        first = (seqs[s] - core + of_core) * rows + which * block
        return pl.ds(pl.multiple_of(first, block), block)

    pieces = [(s, piece, m) for s in (OTHER, OWN) for piece in range(2) for m in (KEY, VALUE)]

    def number_of(s, piece, m):
        return (s * 2 + piece) * 2 + kinds[m]

    def kx_copy(s, piece, m):
        spot = cache.at[kinds[m], place(s, piece, core)]
        at = number_of(s, piece, m)
        return remote(spot, spot, kx_send.at[at], kx_recv.at[at], beside)

    def kd_copy(s, piece, m):
        spot = cache.at[kinds[m], place(s, piece, core)]
        at = number_of(s, piece, m)
        return remote(spot, spot, kd_send.at[at], kd_recv.at[at], partner)

    def settle(s, piece):
        for m in (KEY, VALUE):
            arrived(s, m, piece)
            fresh[kinds[m], s, halves[piece]] = settled(s, m, piece)

        @pl.when(grp == 0)
        def _():
            for m in (KEY, VALUE):
                cache[kinds[m], place(s, piece, core)] = settled(s, m, piece)
            for m in (KEY, VALUE):
                kx_copy(s, piece, m).start()
                kd_copy(s, piece, m).start()

    def relay(s, piece):
        @pl.when(grp != 0)
        def _():
            for m in (KEY, VALUE):
                kx_copy(s, piece, m).wait_recv()
                kd_copy(s, piece, m).start()

    take_z(1)
    for m in (KEY, VALUE):
        send(other, OTHER, halves[0], m)
        launch(partial(OTHER, m, 0))
    for m in (KEY, VALUE):
        keep(other, OTHER, halves[0], m)
    for far in range(2, planes - 1):
        take_z(far)
    settle(OTHER, 0)
    take_z(planes - 1)
    for m in (KEY, VALUE):
        send(other, OTHER, halves[1], m)
        launch(partial(OTHER, m, 1))
    for piece in range(2):
        send(other, OTHER, halves[piece], QUERY)
        launch(partial(OTHER, QUERY, piece))
    for m in (KEY, VALUE):
        keep(other, OTHER, halves[1], m)
    settle(OTHER, 1)
    keep(other, OTHER, everything, QUERY)
    relay(OTHER, 0)
    settle(OWN, 0)
    relay(OTHER, 1)
    settle(OWN, 1)
    for s in (OTHER, OWN):
        for piece in range(2):
            arrived(s, QUERY, piece)
            qbuf[s, halves[piece]] = settled(s, QUERY, piece)
    relay(OWN, 0)
    relay(OWN, 1)
    for s, piece, m in pieces:
        spot = cache.at[kinds[m], place(s, piece, 1 - core)]
        at = number_of(s, piece, m)
        remote(spot, spot, kd_send.at[at], kd_recv.at[at], partner).wait_recv()

    fresh_row = lax.broadcasted_iota(jnp.int32, (block, block), 0)
    fresh_col = lax.broadcasted_iota(jnp.int32, (block, block), 1)
    same = (
        lax.shift_right_logical(fresh_row, step_bits) == lax.shift_right_logical(fresh_col, step_bits)
    ) & (fresh_col <= fresh_row)
    fresh_bias = jnp.where(jnp.where(same, 1 - prompt_one, 0) == 1, 0.0, NEG)
    scale = HD ** (-0.5)

    def attend(s, piece, head):
        at = slice(piece * block, (piece + 1) * block)
        lanes = slice(head * HD, (head + 1) * HD)
        query = qbuf[s, at, lanes]

        def scored(key_block, mask):
            return lax.dot_general(
                query, key_block, contract_last, preferred_element_type=jnp.float32
            ) * scale + mask

        scores = [scored(cache[0, :, lanes], bias[s, at]), scored(fresh[0, s, at, lanes], fresh_bias)]
        values = [cache[1, :, lanes], fresh[1, s, at, lanes]]
        top = jnp.maximum(
            jnp.max(scores[0], axis=1, keepdims=True), jnp.max(scores[1], axis=1, keepdims=True)
        )
        total = jnp.zeros((block, 1), jnp.float32)
        summed = jnp.zeros((block, HD), jnp.float32)
        for score, value in zip(scores, values):
            weight = jnp.exp(score - top)
            total += jnp.sum(weight, axis=1, keepdims=True)
            summed += jnp.dot(weight.astype(jnp.bfloat16), value, preferred_element_type=jnp.float32)
        return (summed / total).astype(jnp.bfloat16)

    def out_copy(piece):
        return remote(osend.at[piece], orecv.at[piece], o_send.at[piece], o_recv.at[piece], across)

    for piece in range(2):
        for head in range(heads):
            osend[piece, :, head * HD : (head + 1) * HD] = attend(OTHER, piece, head)
        launch(out_copy(piece))
    for piece in range(2):
        for head in range(heads):
            lanes = pl.ds(pl.multiple_of(y * half + head * HD, HD), HD)
            out[piece * block : (piece + 1) * block, lanes] = attend(OWN, piece, head)
    for piece in range(2):
        out_copy(piece).wait_recv()
        out[piece * block : (piece + 1) * block, their_heads] = orecv[piece]

    for copy in sent:
        copy.wait_send()
    for step in pieces:
        kd_copy(*step).wait_send()
    for far in range(planes):
        for sub in range(SUBS):

            @pl.when((tp < planes - 1) & (tp >= far))
            def _():
                z_chunk(tp - far, sub, True).wait_send()

            @pl.when((tp > 0) & (tp + far < planes))
            def _():
                z_chunk(tp + far, sub, False).wait_send()

    @pl.when(grp == 0)
    def _():
        for step in pieces:
            kx_copy(*step).wait_send()


def fused(planes, hidden, w_query, w_key, w_value, prompt_len, page_table):
    rows, model = hidden.shape[1:]
    depth, width = w_query.shape
    half = width // 2
    block = rows // 2
    dma = pltpu.SemaphoreType.DMA
    anywhere = pl.BlockSpec(memory_space=pltpu.HBM)
    vmem = pl.BlockSpec(memory_space=pltpu.VMEM)
    result = pl.pallas_call(
        functools.partial(fused_kernel, planes),
        out_shape=jax.ShapeDtypeStruct((rows, width), jnp.bfloat16),
        in_specs=[anywhere] * 6,
        out_specs=vmem,
        scratch_shapes=[
            pltpu.VMEM((1, prompt_len.shape[0]), jnp.int32),
            pltpu.VMEM(page_table.shape[::-1], jnp.int32),
            pltpu.VMEM((rows, 2 * depth), jnp.bfloat16),
            pltpu.VMEM((rows, 2 * depth), jnp.bfloat16),
            pltpu.VMEM((3, 2 * depth, width), jnp.bfloat16),
            pltpu.VMEM((2, 3, rows, half), jnp.float32),
            pltpu.VMEM((2, 2, rows, half), jnp.float32),
            pltpu.VMEM((2, 2, rows, half), jnp.float32),
            pltpu.VMEM((2, rows, half), jnp.bfloat16),
            pltpu.VMEM((2, rows, half), jnp.bfloat16),
            pltpu.VMEM((2, rows, half), jnp.bfloat16),
            pltpu.VMEM((2, 2, rows, half), jnp.bfloat16),
            pltpu.VMEM((2, 4 * rows, half), jnp.bfloat16),
            pltpu.VMEM((2, rows, 4 * rows), jnp.float32),
            pltpu.VMEM((2, block, half), jnp.bfloat16),
            pltpu.VMEM((2, block, half), jnp.bfloat16),
            dma((6,)), dma((3,)), dma((3,)),
            dma((SUBS,)), dma((SUBS,)), dma((planes * SUBS,)), dma((planes * SUBS,)), dma((planes * SUBS,)),
            dma((12,)), dma((12,)),
            dma((8,)), dma((8,)), dma((8,)), dma((8,)),
            dma((2,)), dma((2,)),
        ],
        compiler_params=pltpu.CompilerParams(
            collective_id=0, has_side_effects=True, vmem_limit_bytes=67043328
        ),
    )(hidden, w_query, w_key, w_value, prompt_len.reshape(1, -1), page_table.T)
    return result[None]


def solution(mesh):
    planes = mesh.shape["tp"]
    paired = mesh.shape["grp"] == 2 and mesh.shape["seq"] == 4 and planes == 4
    return jax.shard_map(
        functools.partial(fused, planes) if paired else on_device,
        mesh=mesh,
        in_specs=(P("grp", "seq", None), P("seq", "tp"), P("seq", "tp"), P("seq", "tp"), P(), P()),
        out_specs=P("grp", "seq", "tp"),
        check_vma=False,
    )
```

time: 62.5 us -> 47.3 us (0.76)
  the two profiles are of different devices: /device:TPU:27 before, /device:TPU:0 now
where the time goes in v2:
time: 47.3 us; the launch traced here: 47.2 us
  Pallas kernels  45.5 us (96%)
  local copies, waits for them, and re-layouts  1.67 us (4%)
    pallas_call x1, Pallas kernels, fused(): pl.pallas_call(functools.partial(fused_kernel, planes), out_shape=jax.Sha...  45.5 us
    unnamed x1, local copies, waits for them, and re-layouts  1.67 us

profile of v2, /device:TPU:0, one launch (start us, length us, event | category | flops | bytes accessed | tf_op | source)
XLA Modules:
  0.0 47.2 jit_solution(2048743626783147874)
XLA Ops:
  0.0 45.5 %shard_map.64 = bf16[256,512]{1,0:T(8,128)(2,1)} custom-call(bf16[1,256,4096]{2,1,0:T(8,128)(2,1)} %hidden.1, bf16[1024,512]{1,0:T(8,128)(2,1)} %w_query.1, bf16[1024,512]{1,0:T(8,128)(2,1)} %w_key.1, bf16[1024,512]{1,0:T(8,128)(2,1)} %w_value.1, s32[1,256]{1,0:T(1,128)} %bitcast.5, s32[32,256]{1,0:T(8,128)} %bitcast.4), custom_call_target="tpu_custom_call" | custom-call | tf_op jit(solution)/shard_map/pallas_call | solution.py:515
  45.5 1.7 %copy.8 = bf16[1,256,512]{2,1,0:T(8,128)(2,1)} copy(bf16[1,256,512]{2,1,0:T(8,128)(2,1)} %bitcast.3) | data formatting | bytes 524288

commit v3 on v2

--- a/solution.py
+++ b/solution.py
@@ -174,7 +174,10 @@
     seqs = [2 * y + core, 2 * (1 - y) + core]
     my_heads = pl.ds(pl.multiple_of(y * half, half), half)
     their_heads = pl.ds(pl.multiple_of((1 - y) * half, half), half)
-    halves = [pl.ds(pl.multiple_of(at * block, block), block) for at in (side, 1 - side)]
+    plane_rows = rows // planes
+    starts = (side * block, (planes // 2 - side) * plane_rows, (planes - 1) * (1 - side) * plane_rows)
+    sizes = (block, plane_rows, plane_rows)
+    parts = [pl.ds(pl.multiple_of(start, plane_rows), size) for start, size in zip(starts, sizes)]
 
     def remote(src, dst, send, recv, to):
         return pltpu.make_async_remote_copy(
@@ -298,8 +301,8 @@
         keep(source, s, at, m)
 
     def partial(s, m, piece):
-        at = halves[piece]
-        number = (s * 3 + m) * 2 + piece
+        at = parts[piece]
+        number = (s * 3 + m) * 3 + piece
         return remote(
             part_at(wide_out, value_out, s, m, at), part_at(wide_in, value_in, 1 - s, m, at),
             p_send.at[number], p_recv.at[number], across,
@@ -343,34 +346,34 @@
         swaps[m].wait_recv()
         if at < SUBS:
             take_y(at)
-        for piece in range(2):
-            send(own, OWN, halves[piece], m)
-            launch(partial(OWN, m, piece))
+        for piece in range(3):
+            send(own, OWN, parts[piece], m)
+            if m != QUERY:
+                launch(partial(OWN, m, piece))
         keep(own, OWN, everything, m)
     for sub in range(3, SUBS):
         take_y(sub)
 
     def arrived(s, m, piece):
-        at = halves[piece]
+        at = parts[piece]
         remote(
             part_at(wide_out, value_out, s, m, at), part_at(wide_in, value_in, s, m, at),
-            p_send.at[((1 - s) * 3 + m) * 2 + piece], p_recv.at[((1 - s) * 3 + m) * 2 + piece], across,
+            p_send.at[((1 - s) * 3 + m) * 3 + piece], p_recv.at[((1 - s) * 3 + m) * 3 + piece], across,
         ).wait_recv()
 
     def settled(s, m, piece):
-        at = halves[piece]
+        at = parts[piece]
         far = part_at(wide_in, value_in, s, m, at)[...]
         return (acc[s, m, at] + far.astype(jnp.float32)).astype(jnp.bfloat16)
 
     def place(s, piece, of_core):
-        which = side if piece == 0 else 1 - side
-        first = (seqs[s] - core + of_core) * rows + which * block
-        return pl.ds(pl.multiple_of(first, block), block)
-
-    pieces = [(s, piece, m) for s in (OTHER, OWN) for piece in range(2) for m in (KEY, VALUE)]
+        first = (seqs[s] - core + of_core) * rows + starts[piece]
+        return pl.ds(pl.multiple_of(first, plane_rows), sizes[piece])
+
+    pieces = [(s, piece, m) for s in (OTHER, OWN) for piece in range(3) for m in (KEY, VALUE)]
 
     def number_of(s, piece, m):
-        return (s * 2 + piece) * 2 + kinds[m]
+        return (s * 3 + piece) * 2 + kinds[m]
 
     def kx_copy(s, piece, m):
         spot = cache.at[kinds[m], place(s, piece, core)]
@@ -385,7 +388,7 @@
     def settle(s, piece):
         for m in (KEY, VALUE):
             arrived(s, m, piece)
-            fresh[kinds[m], s, halves[piece]] = settled(s, m, piece)
+            fresh[kinds[m], s, parts[piece]] = settled(s, m, piece)
 
         @pl.when(grp == 0)
         def _():
@@ -402,36 +405,44 @@
                 kx_copy(s, piece, m).wait_recv()
                 kd_copy(s, piece, m).start()
 
+    def others(piece):
+        for m in (KEY, VALUE):
+            send(other, OTHER, parts[piece], m)
+            launch(partial(OTHER, m, piece))
+        for m in (KEY, VALUE):
+            keep(other, OTHER, parts[piece], m)
+
+    def take_query(s):
+        for piece in range(3):
+            arrived(s, QUERY, piece)
+            qbuf[s, parts[piece]] = settled(s, QUERY, piece)
+
     take_z(1)
-    for m in (KEY, VALUE):
-        send(other, OTHER, halves[0], m)
-        launch(partial(OTHER, m, 0))
-    for m in (KEY, VALUE):
-        keep(other, OTHER, halves[0], m)
-    for far in range(2, planes - 1):
-        take_z(far)
+    others(0)
+    take_z(2)
+    others(1)
+    launch(partial(OWN, QUERY, 0))
     settle(OTHER, 0)
-    take_z(planes - 1)
-    for m in (KEY, VALUE):
-        send(other, OTHER, halves[1], m)
-        launch(partial(OTHER, m, 1))
-    for piece in range(2):
-        send(other, OTHER, halves[piece], QUERY)
+    settle(OTHER, 1)
+    settle(OWN, 0)
+    relay(OTHER, 0)
+    take_z(3)
+    others(2)
+    for piece in (1, 2):
+        launch(partial(OWN, QUERY, piece))
+    for piece in range(3):
+        send(other, OTHER, parts[piece], QUERY)
         launch(partial(OTHER, QUERY, piece))
-    for m in (KEY, VALUE):
-        keep(other, OTHER, halves[1], m)
-    settle(OTHER, 1)
-    keep(other, OTHER, everything, QUERY)
-    relay(OTHER, 0)
-    settle(OWN, 0)
+    settle(OTHER, 2)
     relay(OTHER, 1)
     settle(OWN, 1)
-    for s in (OTHER, OWN):
-        for piece in range(2):
-            arrived(s, QUERY, piece)
-            qbuf[s, halves[piece]] = settled(s, QUERY, piece)
+    keep(other, OTHER, everything, QUERY)
+    relay(OTHER, 2)
     relay(OWN, 0)
+    settle(OWN, 2)
     relay(OWN, 1)
+    take_query(OTHER)
+    relay(OWN, 2)
     for s, piece, m in pieces:
         spot = cache.at[kinds[m], place(s, piece, 1 - core)]
         at = number_of(s, piece, m)
@@ -475,6 +486,7 @@
         for head in range(heads):
             osend[piece, :, head * HD : (head + 1) * HD] = attend(OTHER, piece, head)
         launch(out_copy(piece))
+    take_query(OWN)
     for piece in range(2):
         for head in range(heads):
             lanes = pl.ds(pl.multiple_of(y * half + head * HD, HD), HD)
@@ -536,8 +548,8 @@
             pltpu.VMEM((2, block, half), jnp.bfloat16),
             dma((6,)), dma((3,)), dma((3,)),
             dma((SUBS,)), dma((SUBS,)), dma((planes * SUBS,)), dma((planes * SUBS,)), dma((planes * SUBS,)),
-            dma((12,)), dma((12,)),
-            dma((8,)), dma((8,)), dma((8,)), dma((8,)),
+            dma((18,)), dma((18,)),
+            dma((12,)), dma((12,)), dma((12,)), dma((12,)),
             dma((2,)), dma((2,)),
         ],
         compiler_params=pltpu.CompilerParams(

time: 47.3 us -> 46.1 us (0.975)
  Pallas kernels: 45.5 us -> 44.2 us
    pallas_call x1, Pallas kernels: 45.5 us -> 44.2 us  [fused(): pl.pallas_call(functools.partial(fused_kernel, planes), out_shape=jax.Sha...]
where the time goes in v3:
time: 46.1 us; the launch traced here: 45.9 us
  Pallas kernels  44.2 us (96%)
  local copies, waits for them, and re-layouts  1.67 us (4%)
    pallas_call x1, Pallas kernels, fused(): pl.pallas_call(functools.partial(fused_kernel, planes), out_shape=jax.Sha...  44.2 us
    unnamed x1, local copies, waits for them, and re-layouts  1.67 us

profile of v3, /device:TPU:0, one launch (start us, length us, event | category | flops | bytes accessed | tf_op | source)
XLA Modules:
  0.0 45.9 jit_solution(13546023485804064398)
XLA Ops:
  0.0 44.2 %shard_map.64 = bf16[256,512]{1,0:T(8,128)(2,1)} custom-call(bf16[1,256,4096]{2,1,0:T(8,128)(2,1)} %hidden.1, bf16[1024,512]{1,0:T(8,128)(2,1)} %w_query.1, bf16[1024,512]{1,0:T(8,128)(2,1)} %w_key.1, bf16[1024,512]{1,0:T(8,128)(2,1)} %w_value.1, s32[1,256]{1,0:T(1,128)} %bitcast.5, s32[32,256]{1,0:T(8,128)} %bitcast.4), custom_call_target="tpu_custom_call" | custom-call | tf_op jit(solution)/shard_map/pallas_call | solution.py:527
  44.2 1.7 %copy.8 = bf16[1,256,512]{2,1,0:T(8,128)(2,1)} copy(bf16[1,256,512]{2,1,0:T(8,128)(2,1)} %bitcast.3) | data formatting | bytes 524288

commit v4 on v3

--- a/solution.py
+++ b/solution.py
@@ -147,9 +147,9 @@
 
 def fused_kernel(
     planes, hidden, w_query, w_key, w_value, lengths_in, tables_in, out,
-    lengths, tables, own, other, weights, acc, wide_out, wide_in, value_out, value_in, qbuf, fresh, cache, bias, osend, orecv,
+    lengths, tables, stage, own, other, weights, acc, wide_out, wide_in, value_out, value_in, qbuf, fresh, cache, bias, osend, oself,
     local_sem, w_send, w_recv, hy_send, hy_recv, up_send, down_send, hz_recv, p_send, p_recv,
-    kx_send, kx_recv, kd_send, kd_recv, o_send, o_recv,
+    kx_send, kx_recv, kd_send, kd_recv, o_send, o_recv, o_keep,
 ):
     inputs = {QUERY: w_query, KEY: w_key, VALUE: w_value}
     rows = hidden.shape[1]
@@ -192,11 +192,12 @@
     own_keep = pltpu.make_async_copy(
         hidden.at[0, :, pl.ds(pl.multiple_of(y * span, span), span)], own, local_sem.at[5]
     )
-    table_keep.start()
-    length_keep.start()
-    own_keep.start()
-    for m in (KEY, VALUE, QUERY):
-        keeps[m].start()
+    def staged(sub):
+        take = pl.ds(pl.multiple_of((tp * SUBS + sub) * chunk, chunk), chunk)
+        return pltpu.make_async_copy(
+            hidden.at[0, take, pl.ds(pl.multiple_of((1 - y) * span, span), span)], stage.at[sub],
+            local_sem.at[6 + sub],
+        )
 
     barrier = pltpu.get_barrier_semaphore()
     for peer in (across, partner, beside):
@@ -210,6 +211,13 @@
     def _():
         pl.semaphore_signal(barrier, inc=1, device_id=below, device_id_type=pl.DeviceIdType.MESH)
 
+    for sub in range(SUBS):
+        staged(sub).start()
+    for m in (KEY, VALUE, QUERY):
+        keeps[m].start()
+    own_keep.start()
+    table_keep.start()
+    length_keep.start()
     ends = jnp.where(tp == 0, 1, 0) + jnp.where(tp == planes - 1, 1, 0)
     pl.semaphore_wait(barrier, 5 - ends)
 
@@ -219,7 +227,7 @@
     def y_chunk(sub):
         take = chunk_rows(tp, sub)
         return remote(
-            hidden.at[0, take, pl.ds(pl.multiple_of((1 - y) * span, span), span)], other.at[take],
+            stage.at[sub], other.at[take],
             hy_send.at[sub], hy_recv.at[sub], across,
         )
 
@@ -238,11 +246,13 @@
         sent.append(copy)
 
     for sub in range(SUBS):
+        staged(sub).wait()
         launch(y_chunk(sub))
     swaps = {
-        m: remote(inputs[m], weights.at[m, my_depth], w_send.at[m], w_recv.at[m], partner) for m in inputs
+        m: remote(weights.at[m, my_depth], weights.at[m, my_depth], w_send.at[m], w_recv.at[m], partner) for m in inputs
     }
     for m in (KEY, VALUE, QUERY):
+        keeps[m].wait()
         launch(swaps[m])
 
     table_keep.wait()
@@ -342,7 +352,6 @@
 
     own_keep.wait()
     for at, m in enumerate((KEY, VALUE, QUERY)):
-        keeps[m].wait()
         swaps[m].wait_recv()
         if at < SUBS:
             take_y(at)
@@ -480,7 +489,12 @@
         return (summed / total).astype(jnp.bfloat16)
 
     def out_copy(piece):
-        return remote(osend.at[piece], orecv.at[piece], o_send.at[piece], o_recv.at[piece], across)
+        span = pl.ds(piece * block, block)
+        return remote(osend.at[piece], out.at[span, my_heads], o_send.at[piece], o_recv.at[piece], across)
+
+    def out_keep(piece):
+        span = pl.ds(piece * block, block)
+        return pltpu.make_async_copy(oself.at[piece], out.at[span, my_heads], o_keep.at[piece])
 
     for piece in range(2):
         for head in range(heads):
@@ -489,11 +503,12 @@
     take_query(OWN)
     for piece in range(2):
         for head in range(heads):
-            lanes = pl.ds(pl.multiple_of(y * half + head * HD, HD), HD)
-            out[piece * block : (piece + 1) * block, lanes] = attend(OWN, piece, head)
+            oself[piece, :, head * HD : (head + 1) * HD] = attend(OWN, piece, head)
+        out_keep(piece).start()
     for piece in range(2):
-        out_copy(piece).wait_recv()
-        out[piece * block : (piece + 1) * block, their_heads] = orecv[piece]
+        span = pl.ds(piece * block, block)
+        remote(osend.at[piece], out.at[span, their_heads], o_send.at[piece], o_recv.at[piece], across).wait_recv()
+        out_keep(piece).wait()
 
     for copy in sent:
         copy.wait_send()
@@ -523,15 +538,15 @@
     block = rows // 2
     dma = pltpu.SemaphoreType.DMA
     anywhere = pl.BlockSpec(memory_space=pltpu.HBM)
-    vmem = pl.BlockSpec(memory_space=pltpu.VMEM)
     result = pl.pallas_call(
         functools.partial(fused_kernel, planes),
         out_shape=jax.ShapeDtypeStruct((rows, width), jnp.bfloat16),
         in_specs=[anywhere] * 6,
-        out_specs=vmem,
+        out_specs=anywhere,
         scratch_shapes=[
             pltpu.VMEM((1, prompt_len.shape[0]), jnp.int32),
             pltpu.VMEM(page_table.shape[::-1], jnp.int32),
+            pltpu.VMEM((SUBS, rows // planes // SUBS, 2 * depth), jnp.bfloat16),
             pltpu.VMEM((rows, 2 * depth), jnp.bfloat16),
             pltpu.VMEM((rows, 2 * depth), jnp.bfloat16),
             pltpu.VMEM((3, 2 * depth, width), jnp.bfloat16),
@@ -546,11 +561,11 @@
             pltpu.VMEM((2, rows, 4 * rows), jnp.float32),
             pltpu.VMEM((2, block, half), jnp.bfloat16),
             pltpu.VMEM((2, block, half), jnp.bfloat16),
-            dma((6,)), dma((3,)), dma((3,)),
+            dma((6 + SUBS,)), dma((3,)), dma((3,)),
             dma((SUBS,)), dma((SUBS,)), dma((planes * SUBS,)), dma((planes * SUBS,)), dma((planes * SUBS,)),
             dma((18,)), dma((18,)),
             dma((12,)), dma((12,)), dma((12,)), dma((12,)),
-            dma((2,)), dma((2,)),
+            dma((2,)), dma((2,)), dma((2,)),
         ],
         compiler_params=pltpu.CompilerParams(
             collective_id=0, has_side_effects=True, vmem_limit_bytes=67043328

time: 46.1 us -> 45.8 us (level)
  no operation moved by 1% of the time
where the time goes in v4:
time: 45.8 us; the launch traced here: 45.7 us
  Pallas kernels  44 us (96%)
  local copies, waits for them, and re-layouts  1.67 us (4%)
    pallas_call x1, Pallas kernels, fused(): pl.pallas_call(functools.partial(fused_kernel, planes), out_shape=jax.Sha...  44 us
    unnamed x1, local copies, waits for them, and re-layouts  1.67 us

profile of v4, /device:TPU:0, one launch (start us, length us, event | category | flops | bytes accessed | tf_op | source)
XLA Modules:
  0.0 45.7 jit_solution(3763955073860491711)
XLA Ops:
  0.0 44.0 %shard_map.64 = bf16[256,512]{1,0:T(8,128)(2,1)} custom-call(bf16[1,256,4096]{2,1,0:T(8,128)(2,1)} %hidden.1, bf16[1024,512]{1,0:T(8,128)(2,1)} %w_query.1, bf16[1024,512]{1,0:T(8,128)(2,1)} %w_key.1, bf16[1024,512]{1,0:T(8,128)(2,1)} %w_value.1, s32[1,256]{1,0:T(1,128)} %bitcast.5, s32[32,256]{1,0:T(8,128)} %bitcast.4), custom_call_target="tpu_custom_call" | custom-call | tf_op jit(solution)/shard_map/pallas_call | solution.py:541
  44.0 1.7 %copy.8 = bf16[1,256,512]{2,1,0:T(8,128)(2,1)} copy(bf16[1,256,512]{2,1,0:T(8,128)(2,1)} %bitcast.3) | data formatting | bytes 524288

commit v5 on v4

--- a/solution.py
+++ b/solution.py
@@ -431,17 +431,21 @@
     take_z(2)
     others(1)
     launch(partial(OWN, QUERY, 0))
+    launch(partial(OWN, QUERY, 1))
     settle(OTHER, 0)
     settle(OTHER, 1)
     settle(OWN, 0)
     relay(OTHER, 0)
     take_z(3)
-    others(2)
-    for piece in (1, 2):
-        launch(partial(OWN, QUERY, piece))
+    for m in (KEY, VALUE):
+        send(other, OTHER, parts[2], m)
+        launch(partial(OTHER, m, 2))
+    launch(partial(OWN, QUERY, 2))
     for piece in range(3):
         send(other, OTHER, parts[piece], QUERY)
         launch(partial(OTHER, QUERY, piece))
+    for m in (KEY, VALUE):
+        keep(other, OTHER, parts[2], m)
     settle(OTHER, 2)
     relay(OTHER, 1)
     settle(OWN, 1)

time: 45.8 us -> 45.2 us (0.987)
  Pallas kernels: 44 us -> 43.4 us
    pallas_call x1, Pallas kernels: 44 us -> 43.4 us  [fused(): pl.pallas_call(functools.partial(fused_kernel, planes), out_shape=jax.Sha...]
where the time goes in v5:
time: 45.2 us; the launch traced here: 45.1 us
  Pallas kernels  43.4 us (96%)
  local copies, waits for them, and re-layouts  1.67 us (4%)
    pallas_call x1, Pallas kernels, fused(): pl.pallas_call(functools.partial(fused_kernel, planes), out_shape=jax.Sha...  43.4 us
    unnamed x1, local copies, waits for them, and re-layouts  1.67 us

profile of v5, /device:TPU:0, one launch (start us, length us, event | category | flops | bytes accessed | tf_op | source)
XLA Modules:
  0.0 45.1 jit_solution(11972676200258982682)
XLA Ops:
  0.0 43.4 %shard_map.64 = bf16[256,512]{1,0:T(8,128)(2,1)} custom-call(bf16[1,256,4096]{2,1,0:T(8,128)(2,1)} %hidden.1, bf16[1024,512]{1,0:T(8,128)(2,1)} %w_query.1, bf16[1024,512]{1,0:T(8,128)(2,1)} %w_key.1, bf16[1024,512]{1,0:T(8,128)(2,1)} %w_value.1, s32[1,256]{1,0:T(1,128)} %bitcast.5, s32[32,256]{1,0:T(8,128)} %bitcast.4), custom_call_target="tpu_custom_call" | custom-call | tf_op jit(solution)/shard_map/pallas_call | solution.py:545
  43.4 1.7 %copy.8 = bf16[1,256,512]{2,1,0:T(8,128)(2,1)} copy(bf16[1,256,512]{2,1,0:T(8,128)(2,1)} %bitcast.3) | data formatting | bytes 524288
